TPU v7x, 32 devices: a whole 2x2x4 slice. The times are simulated.
32 devices in a mesh: dp: 8 (over z, x), tp: 4 (over y, core).
Axes of the slice: x: 2, y: 2, z: 4, core: 2. Of those that a mesh axis runs over, the one named last changes fastest.
Arguments:
- main: bfloat16 [16512, 1152], P('dp', 'tp'), may hold values from -6 to 6
- long_skip: bfloat16 [16512, 1152], P('dp', 'tp'), may hold values from -6 to 6
- cotangent: bfloat16 [16512, 1152], P('dp', 'tp'), may hold values from -6 to 6
- timesteps: int32 [64], P('dp'), may hold values from 0 to 999
- loss_codes: int32 [64], P('dp'), may hold values from 0 to 7
- code_weights: float32 [8], replicated, may hold values from 0.25 to 4
- item_counts: int32 [8], P('dp'), may hold values from 4 to 8, as said below
- w_skip_main: bfloat16 [1152, 1152], P('tp'), may hold values from -0.125 to 0.125
- w_skip_long: bfloat16 [1152, 1152], P('tp'), may hold values from -0.125 to 0.125
- b_skip: float32 [1152], P('tp'), may hold values from -3 to 3
- ln1_gain: float32 [1152], P('tp'), may hold values from 0.25 to 1.75
- ln1_bias: float32 [1152], P('tp'), may hold values from -2.4 to 2.4
- w_qkv: bfloat16 [3, 1152, 1152], P(None, None, 'tp'), may hold values from -0.1875 to 0.1875
- w_proj: bfloat16 [1152, 1152], P('tp'), may hold values from -1.5 to 1.5
- b_proj: float32 [1152], P('tp'), may hold values from -3 to 3
- ln2_gain: float32 [1152], P('tp'), may hold values from 0.25 to 1.75
- ln2_bias: float32 [1152], P('tp'), may hold values from -2.4 to 2.4
- w_up: bfloat16 [1152, 4608], P(None, 'tp'), may hold values from -0.1875 to 0.1875
- b_up: float32 [4608], P('tp'), may hold values from -3 to 3
- w_down: bfloat16 [4608, 1152], P('tp'), may hold values from -0.09375 to 0.09375
- b_down: float32 [1152], P('tp'), may hold values from -3 to 3
Outputs:
- out: bfloat16 [16512, 1152], P('dp', 'tp')
- d_main: bfloat16 [16512, 1152], P('dp', 'tp')
- d_long: bfloat16 [16512, 1152], P('dp', 'tp')
- g_w_skip_main: float32 [1152, 1152], P('tp')
- g_w_skip_long: float32 [1152, 1152], P('tp')
- g_b_skip: float32 [1152], P('tp')
- g_ln1_gain: float32 [1152], P('tp')
- g_ln1_bias: float32 [1152], P('tp')
- g_w_qkv: float32 [3, 1152, 1152], P(None, None, 'tp')
- g_w_proj: float32 [1152, 1152], P('tp')
- g_b_proj: float32 [1152], P('tp')
- g_ln2_gain: float32 [1152], P('tp')
- g_ln2_bias: float32 [1152], P('tp')
- g_w_up: float32 [1152, 4608], P(None, 'tp')
- g_b_up: float32 [4608], P('tp')
- g_w_down: float32 [4608, 1152], P('tp')
- g_b_down: float32 [1152], P('tp')
Inputs may be any that keep to these rules, and one draw needn't show every extreme that they name: `item_counts`: each batch group holds 4 to 8 items; some group is full and some holds exactly 4.
All inputs are finite; a program needn't handle non-finite values.
Results may differ from a plain program's by a relative error of at most 0.02.
Values may be sent and summed in bfloat16 or wider, within the bound.
A program may use at most 192 MiB of HBM per device.

v0:
```python
import math
import jax
import jax.numpy as jnp
from jax import lax
from jax.sharding import PartitionSpec as P

HEAD = 72
SEQ = 258
TSTEPS = 1000
EPSILON = 1e-06
ROOT_HALF = 0.7071067811865476
DENSITY_SCALE = 0.3989422804014327


def item_factors(timesteps, loss_codes, code_weights, group_items):
    steps_float = timesteps.astype(jnp.float32)
    phase = (steps_float / TSTEPS + 0.008) / 1.008 * (math.pi / 2.0)
    cosine = jnp.cos(phase)
    signal = cosine * cosine
    weight = jnp.minimum(1.0, 5.0 * (1.0 - signal) / signal)
    picks = (
        loss_codes[:, None] == jnp.arange(code_weights.shape[0], dtype=jnp.int32)[None, :]
    ).astype(jnp.float32)
    coded = jnp.sum(picks * code_weights[None, :], axis=1)
    valid = (jnp.arange(timesteps.shape[0], dtype=jnp.int32) < group_items).astype(jnp.float32)
    return (weight * coded * valid, valid)


def layer_norm(stream, gain, bias, width):
    totals, squares = lax.psum((jnp.sum(stream, 0), jnp.sum(stream * stream, 0)), "tp")
    mean = totals / width
    rstd = lax.rsqrt(squares / width - mean * mean + EPSILON)
    normed = (stream - mean[None, :]) * rstd[None, :]
    rounded = (normed * gain[:, None] + bias[:, None]).astype(jnp.bfloat16)
    return (normed, rstd, lax.all_gather(rounded, "tp", axis=0, tiled=True))


def norm_back(d_normed, normed, rstd, gain, width):
    g_gain = jnp.sum(d_normed * normed, 1)
    g_bias = jnp.sum(d_normed, 1)
    scaled = d_normed * gain[:, None]
    first, second = lax.psum((jnp.sum(scaled, 0), jnp.sum(scaled * normed, 0)), "tp")
    back = rstd[None, :] * (scaled - first[None, :] / width - normed * second[None, :] / width)
    return (back, g_gain, g_bias)


def reduce_back(term, local_width):
    return lax.psum_scatter(
        term(jnp.int32(0), lax.axis_size("tp") * local_width).astype(jnp.bfloat16),
        "tp",
        scatter_dimension=0,
        tiled=True,
    ).astype(jnp.float32)


def fold_back(shard, pairs):
    piece = lax.all_gather(shard, "tp", axis=0, tiled=True)
    new_acts = tuple(
        (
            jnp.einsum("fc,ct->ft", weight, piece, preferred_element_type=jnp.float32)
            for weight, acts in pairs
        )
    )
    new_weights = tuple(
        (
            jnp.einsum("ft,ct->fc", acts, piece, preferred_element_type=jnp.float32)
            for weight, acts in pairs
        )
    )
    return (new_acts, new_weights)


def split_heads(flat, heads_here):
    pair_count = flat.shape[1] // (2 * SEQ)
    shaped = flat.reshape(heads_here, HEAD, pair_count, 2, SEQ)
    return jnp.moveaxis(shaped, 2, 0)


def join_heads(blocks):
    moved = jnp.moveaxis(blocks, 0, 2)
    return moved.reshape(moved.shape[0] * moved.shape[1], -1)


def attend(block):
    query_rows, key_rows, value_rows = block
    scale = 1.0 / math.sqrt(HEAD)
    scores = (
        jnp.einsum("hdbi,hdbj->hbij", query_rows, key_rows, preferred_element_type=jnp.float32)
        * scale
    )
    peak = jnp.max(scores, axis=-1, keepdims=True)
    logsum = peak + jnp.log(jnp.sum(jnp.exp(scores - peak), axis=-1, keepdims=True))
    probs = jnp.exp(scores - logsum).astype(jnp.bfloat16)
    attended = jnp.einsum("hbij,hdbj->hdbi", probs, value_rows, preferred_element_type=jnp.float32)
    return (attended.astype(jnp.bfloat16), logsum[..., 0])


def attend_back(block):
    query_rows, key_rows, value_rows, logsum, d_attended = block
    scale = 1.0 / math.sqrt(HEAD)
    scores = (
        jnp.einsum("hdbi,hdbj->hbij", query_rows, key_rows, preferred_element_type=jnp.float32)
        * scale
    )
    probs = jnp.exp(scores - logsum[..., None])
    probs_low = probs.astype(jnp.bfloat16)
    d_probs = jnp.einsum(
        "hdbi,hdbj->hbij", d_attended, value_rows, preferred_element_type=jnp.float32
    )
    delta = jnp.sum(probs * d_probs, axis=-1, keepdims=True)
    d_scores = (probs * (d_probs - delta)).astype(jnp.bfloat16)
    d_query = (
        jnp.einsum("hbij,hdbj->hdbi", d_scores, key_rows, preferred_element_type=jnp.float32)
        * scale
    )
    d_key = (
        jnp.einsum("hbij,hdbi->hdbj", d_scores, query_rows, preferred_element_type=jnp.float32)
        * scale
    )
    d_value = jnp.einsum(
        "hbij,hdbi->hdbj", probs_low, d_attended, preferred_element_type=jnp.float32
    )
    return (d_query.astype(jnp.bfloat16), d_key.astype(jnp.bfloat16), d_value.astype(jnp.bfloat16))


def body(
    main,
    long_skip,
    cotangent,
    timesteps,
    loss_codes,
    code_weights,
    item_counts,
    w_skip_main,
    w_skip_long,
    b_skip,
    ln1_gain,
    ln1_bias,
    w_qkv,
    w_proj,
    b_proj,
    ln2_gain,
    ln2_bias,
    w_up,
    b_up,
    w_down,
    b_down,
):
    local_width = main.shape[1]
    width = w_skip_main.shape[1]
    heads_here = local_width // HEAD
    item_scale, valid = item_factors(timesteps, loss_codes, code_weights, item_counts[0])
    row_scale = jnp.repeat(item_scale, SEQ)
    row_valid = jnp.repeat(valid, SEQ)
    main_cols = main.T
    long_cols = long_skip.T
    stream = (
        lax.psum_scatter(
            jnp.einsum("dc,dt->ct", w_skip_main, main_cols, preferred_element_type=jnp.float32)
            + jnp.einsum("dc,dt->ct", w_skip_long, long_cols, preferred_element_type=jnp.float32),
            "tp",
            scatter_dimension=0,
            tiled=True,
        )
        + b_skip[:, None]
    )
    normed_one, rstd_one, full_one = layer_norm(stream, ln1_gain, ln1_bias, width)
    qkv = jnp.einsum("edc,dt->ect", w_qkv, full_one, preferred_element_type=jnp.float32).astype(
        jnp.bfloat16
    )
    query_blocks = split_heads(qkv[0], heads_here)
    key_blocks = split_heads(qkv[1], heads_here)
    value_blocks = split_heads(qkv[2], heads_here)
    attended_blocks, logsums = lax.map(attend, (query_blocks, key_blocks, value_blocks))
    attended = join_heads(attended_blocks)
    cols_here = w_proj
    projected = lax.psum_scatter(
        jnp.einsum("rc,rt->ct", cols_here, attended, preferred_element_type=jnp.float32).astype(
            jnp.bfloat16
        ),
        "tp",
        scatter_dimension=0,
        tiled=True,
    ).astype(jnp.float32)
    stream_two = stream + projected + b_proj[:, None]
    normed_two, rstd_two, full_two = layer_norm(stream_two, ln2_gain, ln2_bias, width)
    upward = (
        jnp.einsum("dc,dt->ct", w_up, full_two, preferred_element_type=jnp.float32) + b_up[:, None]
    )
    activated = jax.nn.gelu(upward, approximate=False).astype(jnp.bfloat16)
    cols_here = w_down
    result = (
        stream_two
        + lax.psum_scatter(
            jnp.einsum(
                "fc,ft->ct", cols_here, activated, preferred_element_type=jnp.float32
            ).astype(jnp.bfloat16),
            "tp",
            scatter_dimension=0,
            tiled=True,
        ).astype(jnp.float32)
        + b_down[:, None]
    )
    out = (result * row_valid[None, :]).T.astype(jnp.bfloat16)
    grad_low = (cotangent.T.astype(jnp.float32) * row_scale[None, :]).astype(jnp.bfloat16)
    grad_wide = grad_low.astype(jnp.float32)
    g_b_down = jnp.sum(grad_wide, 1)
    (d_activated,), (g_w_down,) = fold_back(grad_low, ((w_down, activated),))
    cumulative = 0.5 * (1.0 + lax.erf(upward * ROOT_HALF))
    density = jnp.exp(-0.5 * upward * upward) * DENSITY_SCALE
    d_upward = (d_activated * (cumulative + upward * density)).astype(jnp.bfloat16)
    g_b_up = jnp.sum(d_upward.astype(jnp.float32), 1)
    g_w_up = jnp.einsum("dt,ft->df", full_two, d_upward, preferred_element_type=jnp.float32)

    def up_term(start, count_rows):
        return jnp.einsum("cf,ft->ct", w_up, d_upward, preferred_element_type=jnp.float32)

    d_normed_two = reduce_back(up_term, local_width)
    back_two, g_ln2_gain, g_ln2_bias = norm_back(
        d_normed_two, normed_two, rstd_two, ln2_gain, width
    )
    d_stream_two = (back_two + grad_wide).astype(jnp.bfloat16)
    d_stream_wide = d_stream_two.astype(jnp.float32)
    g_b_proj = jnp.sum(d_stream_wide, 1)
    (d_attended,), (g_w_proj,) = fold_back(d_stream_two, ((w_proj, attended),))
    d_attended_blocks = split_heads(d_attended.astype(jnp.bfloat16), heads_here)
    d_queries, d_keys, d_values = lax.map(
        attend_back, (query_blocks, key_blocks, value_blocks, logsums, d_attended_blocks)
    )
    d_qkv = jnp.stack([join_heads(d_queries), join_heads(d_keys), join_heads(d_values)], axis=0)
    g_w_qkv = jnp.einsum("dt,ect->edc", full_one, d_qkv, preferred_element_type=jnp.float32)

    def qkv_term(start, count_rows):
        return jnp.einsum("ecr,ert->ct", w_qkv, d_qkv, preferred_element_type=jnp.float32)

    d_normed_one = reduce_back(qkv_term, local_width)
    back_one, g_ln1_gain, g_ln1_bias = norm_back(
        d_normed_one, normed_one, rstd_one, ln1_gain, width
    )
    d_stream = (back_one + d_stream_wide).astype(jnp.bfloat16)
    g_b_skip = jnp.sum(d_stream.astype(jnp.float32), 1)
    (d_main_cols, d_long_cols), (g_w_main, g_w_long) = fold_back(
        d_stream, ((w_skip_main, main_cols), (w_skip_long, long_cols))
    )
    (
        g_w_main,
        g_w_long,
        g_b_skip,
        g_ln1_gain,
        g_ln1_bias,
        g_w_qkv,
        g_w_proj,
        g_b_proj,
        g_ln2_gain,
        g_ln2_bias,
        g_w_up,
        g_b_up,
        g_w_down,
        g_b_down,
    ) = (
        lax.psum(g_w_main.astype(jnp.bfloat16), "dp").astype(jnp.float32),
        lax.psum(g_w_long.astype(jnp.bfloat16), "dp").astype(jnp.float32),
        lax.psum(g_b_skip.astype(jnp.bfloat16), "dp").astype(jnp.float32),
        lax.psum(g_ln1_gain.astype(jnp.bfloat16), "dp").astype(jnp.float32),
        lax.psum(g_ln1_bias.astype(jnp.bfloat16), "dp").astype(jnp.float32),
        lax.psum(g_w_qkv.astype(jnp.bfloat16), "dp").astype(jnp.float32),
        lax.psum(g_w_proj.astype(jnp.bfloat16), "dp").astype(jnp.float32),
        lax.psum(g_b_proj.astype(jnp.bfloat16), "dp").astype(jnp.float32),
        lax.psum(g_ln2_gain.astype(jnp.bfloat16), "dp").astype(jnp.float32),
        lax.psum(g_ln2_bias.astype(jnp.bfloat16), "dp").astype(jnp.float32),
        lax.psum(g_w_up.astype(jnp.bfloat16), "dp").astype(jnp.float32),
        lax.psum(g_b_up.astype(jnp.bfloat16), "dp").astype(jnp.float32),
        lax.psum(g_w_down.astype(jnp.bfloat16), "dp").astype(jnp.float32),
        lax.psum(g_b_down.astype(jnp.bfloat16), "dp").astype(jnp.float32),
    )
    d_main = d_main_cols.T.astype(jnp.bfloat16)
    d_long = d_long_cols.T.astype(jnp.bfloat16)
    return (
        out,
        d_main,
        d_long,
        g_w_main,
        g_w_long,
        g_b_skip,
        g_ln1_gain,
        g_ln1_bias,
        g_w_qkv,
        g_w_proj,
        g_b_proj,
        g_ln2_gain,
        g_ln2_bias,
        g_w_up,
        g_b_up,
        g_w_down,
        g_b_down,
    )


def solution(mesh):
    return jax.shard_map(
        body,
        mesh=mesh,
        in_specs=(
            P("dp", "tp"),
            P("dp", "tp"),
            P("dp", "tp"),
            P("dp"),
            P("dp"),
            P(),
            P("dp"),
            P("tp", None),
            P("tp", None),
            P("tp"),
            P("tp"),
            P("tp"),
            P(None, None, "tp"),
            P("tp", None),
            P("tp"),
            P("tp"),
            P("tp"),
            P(None, "tp"),
            P("tp"),
            P("tp", None),
            P("tp"),
        ),
        out_specs=(
            P("dp", "tp"),
            P("dp", "tp"),
            P("dp", "tp"),
            P("tp", None),
            P("tp", None),
            P("tp"),
            P("tp"),
            P("tp"),
            P(None, None, "tp"),
            P("tp", None),
            P("tp"),
            P("tp"),
            P("tp"),
            P(None, "tp"),
            P("tp"),
            P("tp", None),
            P("tp"),
        ),
        check_vma=False,
    )
```

profile of v0, /device:TPU:0, one launch (start us, length us, event | category | flops | bytes accessed | tf_op | source)
XLA Modules:
  0.0 1135.2 jit_solution(10548227006924629064)
XLA Ops:
  7.3 4.6 fusion.123
  11.9 6.9 convolution_add_fusion
  18.9 84.4 %reduce-scatter.16.cloned.1.call-done = f32[288,2064]{1,0:T(8,128)} async-done(((f32[1152,2064]{1,0:T(8,128)}), f32[288,2064]{1,0:T(8,128)}) %reduce-scatter.16.cloned.1.call-update) | async-done | bytes 2377744
  109.4 10.3 all-reduce.3
  126.7 39.5 %all-gather.6.cloned.1.call-done = bf16[1152,2064]{1,0:T(8,128)(2,1)} async-done(((bf16[288,2064]{1,0:T(8,128)(2,1)}), bf16[1152,2064]{1,0:T(8,128)(2,1)}) %all-gather.6.cloned.1.call-update) | async-done | bytes 4755472 | tf_op jit(solution)/shard_map/all_gather | solution.py:35
  166.2 8.2 fusion.83
  176.4 6.6 reshape_squeeze.11
  183.0 6.6 reshape_squeeze.10
  189.6 6.6 reshape_squeeze.9
  203.0 23.4 %while.26 = (s32[]{:T(128)}, bf16[4,4,72,2,258]{4,2,3,1,0:T(8,128)(2,1)}, f32[4,4,2,258]{3,2,1,0:T(2,128)}, bf16[4,4,72,2,258]{4,2,3,1,0:T(8,128)(2,1)}, bf16[4,...) while((s32[]{:T(128)}, bf16[4,4,72,2,258]{4,2,3,1,0:T(8,128)(2,1)}, ...), condition=%wide.region_8.0_spmd, body=%wide.region_5.8_spmd.sunk | while | flops 157770096 | bytes 8231833 | solution.py:174
  230.5 5.1 reshape.91
  235.6 6.4 fusion.62
  242.0 8.4 copy.129
  250.5 50.0 %reduce-scatter.18.cloned.1.call-done = bf16[288,2064]{1,0:T(8,128)(2,1)} async-done(((bf16[1152,2064]{1,0:T(8,128)(2,1)}), bf16[288,2064]{1,0:T(8,128)(2,1)}) %reduce-scatter.18.cloned.1.call-update) | async-done | bytes 1188880
  303.0 4.6 fusion.116
  307.6 10.3 all-reduce.2
  333.6 30.3 %all-gather.8.cloned.1.call-done = bf16[1152,2064]{1,0:T(8,128)(2,1)} async-done(((bf16[288,2064]{1,0:T(8,128)(2,1)}), bf16[1152,2064]{1,0:T(8,128)(2,1)}) %all-gather.8.cloned.1.call-update) | async-done | bytes 4755472 | tf_op jit(solution)/shard_map/all_gather | solution.py:35
  363.9 32.2 %fusion.68 = (bf16[1152,2064]{0,1:T(8,128)(2,1)S(1)}, f32[1152,2064]{0,1:T(8,128)}) fusion(f32[1152]{0:T(1024)S(1)} %copy-done.46, bf16[1152,2064]{1,0:T(8,128)(2,1)} %all-gather.8.cloned.1.call-done, bf16[1152,1152]{1,0:T(8,128)(2,1)S(1)} %copy-done), kind=kOutput, calls=%fused_computation.81 | convolution fusion | flops 5635215360 | bytes 21680640 | tf_op jit(solution)/shard_map/dc,dt->ct/dot_general | solution.py:188
  398.4 8.5 fusion.63
  406.9 8.4 copy.131
  415.3 16.6 %fusion.122 = (bf16[1152]{0:T(1024)(128)(2,1)}, bf16[1152,2064]{0,1:T(8,128)(2,1)S(1)}) fusion(f32[1152,2064]{0,1:T(8,128)} %get-tuple-element.220, bf16[1152,2064]{1,0:T(8,128)(2,1)} %all-gather.10.cloned.1.call-done, bf16[1152,1152]{1,0:T(8,128)(2,1)} %param.44), kind=kOutput, calls=%fused_computation.176 | convolution fusion | flops 5504439296 | bytes 21678336 | tf_op jit(solution)/shard_map/fc,ct->ft/dot_general | solution.py:60
  434.1 8.7 fusion.64
  442.8 8.4 copy.133
  451.4 13.8 %reduce-scatter.20.cloned.1.call-done = bf16[288,2064]{1,0:T(8,128)(2,1)} async-done(((bf16[1152,2064]{1,0:T(8,128)(2,1)}), bf16[288,2064]{1,0:T(8,128)(2,1)}) %reduce-scatter.20.cloned.1.call-update) | async-done | bytes 1188880
  467.8 50.5 %reduce-scatter.22.cloned.1.call-done = bf16[288,2064]{1,0:T(8,128)(2,1)} async-done(((bf16[1152,2064]{1,0:T(8,128)(2,1)}), bf16[288,2064]{1,0:T(8,128)(2,1)}) %reduce-scatter.22.cloned.1.call-update) | async-done | bytes 1188880
  520.9 6.0 fusion.101
  526.9 10.3 all-reduce.1
  537.2 5.0 fusion.117
  544.9 39.8 %all-gather.12.cloned.1.call-done = bf16[1152,2064]{1,0:T(8,128)(2,1)} async-done(((bf16[288,2064]{1,0:T(8,128)(2,1)}), bf16[1152,2064]{1,0:T(8,128)(2,1)}) %all-gather.12.cloned.1.call-update) | async-done | bytes 4755472 | tf_op jit(solution)/shard_map/all_gather | solution.py:57
  584.7 5.3 fusion.92
  590.0 6.2 reshape.92
  601.7 51.3 %while.27 = (s32[]{:T(128)}, bf16[4,4,72,2,258]{4,2,3,1,0:T(8,128)(2,1)}, bf16[4,4,72,2,258]{4,2,3,1,0:T(8,128)(2,1)}, bf16[4,4,72,2,258]{4,2,3,1,0:T(8,128)(2,1...) while((s32[]{:T(128)}, ...), condition=%wide.region_23.24_spmd, body=%wide.region_21.23_spmd.sunk | while | flops 390539744 | bytes 20462064 | solution.py:227
  662.1 5.3 stack_reshape.9
  669.9 5.2 stack_reshape.10
  678.8 7.7 fusion.65
  686.5 8.4 copy.135
  695.0 50.0 %reduce-scatter.24.cloned.1.call-done = bf16[288,2064]{1,0:T(8,128)(2,1)} async-done(((bf16[1152,2064]{1,0:T(8,128)(2,1)}), bf16[288,2064]{1,0:T(8,128)(2,1)}) %reduce-scatter.24.cloned.1.call-update) | async-done | bytes 1188880
  751.9 10.5 all-reduce
  762.4 5.1 fusion.119
  770.1 11.5 %convolution_convert_fusion.4 = bf16[1152,1152]{1,0:T(8,128)(2,1)} fusion(bf16[1152,2064]{1,0:T(8,128)(2,1)} %all-gather.8.cloned.1.call-done, bf16[1152,2064]{0,1:T(8,128)(2,1)} %copy-done.49), kind=kOutput, calls=%fused_computation.102 | convolution fusion | flops 5479612416 | bytes 12165120 | tf_op jit(solution)/shard_map/dt,ft->df/dot_general | solution.py:213
  781.6 12.4 %convolution_convert_fusion.3 = bf16[1152,1152]{1,0:T(8,128)(2,1)} fusion(bf16[1152,2064]{0,1:T(8,128)(2,1)} %copy-done.50, bf16[1152,2064]{1,0:T(8,128)(2,1)} %all-gather.10.cloned.1.call-done), kind=kOutput, calls=%fused_computation.101 | convolution fusion | flops 5479612416 | bytes 12165120 | tf_op jit(solution)/shard_map/ft,ct->fc/dot_general | solution.py:66
  796.9 6.9 fusion.108
  803.8 6.2 all-gather.14.cloned.1.call-done
  810.0 5.3 fusion.112
  823.3 39.2 %all-reduce.4 = (bf16[288]{0:T(512)(128)(2,1)S(1)}, bf16[288]{0:T(512)(128)(2,1)S(1)}, bf16[288]{0:T(512)(128)(2,1)S(1)}, bf16[288]{0:T(512)(128)(2,1)S(1)}, bf1...) all-reduce(bf16[288]{0:T(512)(128)(2,1)S(1)} %get-tuple-element.204, ...), channel_id=1, replica_groups=mesh['dp'=8,'tp'=4] {'dp'}, use_global_device_ids=true, to_apply=%region_32.33 | all-reduce | flops 3168 | bytes 12672 | tf_op jit(solution)/shard_map/psum | solution.py:263
  867.1 5.4 convolution_convert_fusion.7
  872.6 5.3 convolution_convert_fusion.6
  877.9 235.9 %all-reduce.8.cloned.1.call-done = (bf16[288,1152]{1,0:T(8,128)(2,1)}, bf16[288,1152]{1,0:T(8,128)(2,1)}, bf16[3,1152,288]{1,2,0:T(8,128)(2,1)}, bf16[288,1152]{...) async-done(((bf16[288,1152]{1,0:T(8,128)(2,1)}, bf16[288,1152]{1,0:T(8,128)(2,1)}, bf16[3,1152,288]{1,2,0:T(8,128)(2,1)}, ...) | async-done | bytes 9289744 | tf_op jit(solution)/shard_map/psum | solution.py:261
  (243 shorter events, 190.7 us)
Async XLA Ops:
  7.2 356.7 %copy-start = (bf16[1152,1152]{1,0:T(8,128)(2,1)S(1)}, bf16[1152,1152]{1,0:T(8,128)(2,1)}, u32[]{:S(2)}) copy-start(bf16[1152,1152]{1,0:T(8,128)(2,1)} %param.42) | copy-start | bytes 7962628
  7.2 4.6 copy-start.15
  7.2 96.1 %reduce-scatter.16.cloned.1.call-start = ((), (), s32[]{:S(2)}) async-start(), calls=%async_computation.10 | async-start | bytes 12533760
  7.3 4.6 copy-start.20
  18.8 88.0 %copy-start.30 = (f32[288]{0:T(512)S(1)}, f32[288]{0:T(512)}, u32[]{:S(2)}) copy-start(f32[288]{0:T(512)} %param.34) | copy-start | bytes 3460
  18.8 101.5 %copy-start.33 = (f32[288]{0:T(512)S(1)}, f32[288]{0:T(512)}, u32[]{:S(2)}) copy-start(f32[288]{0:T(512)} %param.35) | copy-start | bytes 3460
  18.9 101.5 %copy-start.36 = (f32[288]{0:T(512)S(1)}, f32[288]{0:T(512)}, u32[]{:S(2)}) copy-start(f32[288]{0:T(512)} %param.36) | copy-start | bytes 3460
  18.9 147.4 %all-gather.6.cloned.1.call-start = ((), (), s32[]{:S(2)}) async-start(), calls=%async_computation.5 | async-start | bytes 6266880 | tf_op jit(solution)/shard_map/all_gather | solution.py:35
  126.4 174.0 %reduce-scatter.18.cloned.1.call-start = ((), (), s32[]{:S(2)}) async-start(), calls=%async_computation.11 | async-start | bytes 6266880
  226.4 9.2 copy-start.44
  250.4 52.6 %copy-start.37 = (f32[288]{0:T(512)S(1)}, f32[288]{0:T(512)}, u32[]{:S(2)}) copy-start(f32[288]{0:T(512)} %param.39) | copy-start | bytes 3460
  250.4 113.5 %all-gather.8.cloned.1.call-start = ((), (), s32[]{:S(2)}) async-start(), calls=%async_computation.6 | async-start | bytes 6266880 | tf_op jit(solution)/shard_map/all_gather | solution.py:35
  303.0 14.9 %copy-start.32 = (f32[288]{0:T(512)S(1)}, f32[288]{0:T(512)}, u32[]{:S(2)}) copy-start(f32[288]{0:T(512)} %param.40) | copy-start | bytes 3460
  303.0 14.9 %copy-start.38 = (f32[288]{0:T(512)S(1)}, f32[288]{0:T(512)}, u32[]{:S(2)}) copy-start(f32[288]{0:T(512)} %param.41) | copy-start | bytes 3460
  321.4 3.5 copy-start.40
  324.0 91.3 %all-gather.10.cloned.1.call-start = ((), (), s32[]{:S(2)}) async-start(), calls=%async_computation.7 | async-start | bytes 6266880 | tf_op jit(solution)/shard_map/all_gather | solution.py:57
  328.0 35.9 %copy-start.46 = (f32[1152]{0:T(1024)S(1)}, f32[1152]{0:T(1024)}, u32[]{:S(2)}) copy-start(f32[1152]{0:T(1024)} %param.43) | copy-start | bytes 13828
  333.6 131.7 %reduce-scatter.20.cloned.1.call-start = ((), (), s32[]{:S(2)}) async-start(), calls=%async_computation.12 | async-start | bytes 6266880
  363.9 34.5 %copy-start.42 = (bf16[1152,1152]{1,0:T(8,128)(2,1)S(1)}, bf16[1152,1152]{1,0:T(8,128)(2,1)}, u32[]{:S(2)}) copy-start(bf16[1152,1152]{1,0:T(8,128)(2,1)} %param.44) | copy-start | bytes 7962628
  415.3 103.1 %reduce-scatter.22.cloned.1.call-start = ((), (), s32[]{:S(2)}) async-start(), calls=%async_computation.13 | async-start | bytes 6266880
  451.2 69.7 %copy-start.39 = (f32[288]{0:T(512)S(1)}, f32[288]{0:T(512)}, u32[]{:S(2)}) copy-start(f32[288]{0:T(512)} %param.45) | copy-start | bytes 3460
  451.2 133.4 %all-gather.12.cloned.1.call-start = ((), (), s32[]{:S(2)}) async-start(), calls=%async_computation.8 | async-start | bytes 6266880 | tf_op jit(solution)/shard_map/all_gather | solution.py:57
  520.9 16.3 %copy-start.2 = (bf16[2064,288]{1,0:T(8,128)(2,1)S(1)}, bf16[2064,288]{1,0:T(8,128)(2,1)}, u32[]{:S(2)}) copy-start(bf16[2064,288]{1,0:T(8,128)(2,1)} %copy.114) | copy-start | bytes 3566596
  542.2 42.5 %copy-start.45 = (bf16[288,1152]{1,0:T(8,128)(2,1)S(1)}, bf16[288,1152]{1,0:T(8,128)(2,1)}, u32[]{:S(2)}) copy-start(bf16[288,1152]{1,0:T(8,128)(2,1)} %param.38) | copy-start | bytes 1990660
  544.8 200.1 %reduce-scatter.24.cloned.1.call-start = ((), (), s32[]{:S(2)}) async-start(), calls=%async_computation.14 | async-start | bytes 6266880
  657.9 9.4 copy-start.7
  669.9 5.2 copy-start.9
  675.1 3.7 copy-start.43
  694.9 52.6 %copy-start.27 = (f32[2064]{0:T(1024)S(1)}, f32[2064]{0:T(1024)}, u32[]{:S(2)}) copy-start(f32[2064]{0:T(1024)} %copy-done.26) | copy-start | bytes 24772
  694.9 52.6 %copy-start.29 = (f32[2064]{0:T(1024)S(1)}, f32[2064]{0:T(1024)}, u32[]{:S(2)}) copy-start(f32[2064]{0:T(1024)} %copy-done.28) | copy-start | bytes 24772
  694.9 52.6 %copy-start.31 = (f32[288]{0:T(512)S(1)}, f32[288]{0:T(512)}, u32[]{:S(2)}) copy-start(f32[288]{0:T(512)} %param.34) | copy-start | bytes 3460
  694.9 52.6 %copy-start.34 = (f32[288]{0:T(512)S(1)}, f32[288]{0:T(512)}, u32[]{:S(2)}) copy-start(f32[288]{0:T(512)} %param.35) | copy-start | bytes 3460
  694.9 67.5 %copy-start.4 = (bf16[288,2064]{0,1:T(8,128)(2,1)S(1)}, bf16[288,2064]{0,1:T(8,128)(2,1)}, u32[]{:S(2)}) copy-start(bf16[288,2064]{0,1:T(8,128)(2,1)} %get-tuple-element.203) | copy-start | bytes 3566596
  694.9 115.0 %all-gather.14.cloned.1.call-start = ((), (), s32[]{:S(2)}) async-start(), calls=%async_computation.9 | async-start | bytes 6266880 | tf_op jit(solution)/shard_map/all_gather | solution.py:57
  770.1 343.8 %all-reduce.8.cloned.1.call-start = ((), (), s32[]{:S(2)}) async-start(), calls=%async_computation.15 | async-start | bytes 18579456 | tf_op jit(solution)/shard_map/psum | solution.py:261
  770.1 23.9 %slice-start.2 = ((s8[5013504]{0:T(1024)(128)(4,1)}), s8[4194304]{0:T(1024)(128)(4,1)S(1)}, s32[]{:S(2)}) async-start(s8[5013504]{0:T(1024)(128)(4,1)} %bitcast.211), calls=%async_computation.18 | async-start | bytes 8388608
  770.1 26.8 %slice-start = ((s8[5013504]{0:T(1024)(128)(4,1)}), s8[4194304]{0:T(1024)(128)(4,1)S(1)}, s32[]{:S(2)}) async-start(s8[5013504]{0:T(1024)(128)(4,1)} %bitcast.209), calls=%async_computation.16 | async-start | bytes 8388608
  781.6 12.4 %copy-start.18 = (bf16[288,2064]{1,0:T(8,128)(2,1)S(1)}, bf16[288,2064]{1,0:T(8,128)(2,1)}, u32[]{:S(2)}) copy-start(bf16[288,2064]{1,0:T(8,128)(2,1)} %reshape.91) | copy-start | bytes 3566596
  781.6 12.4 %slice-start.3 = ((s8[5013504]{0:T(1024)(128)(4,1)}), s8[819200]{0:T(1024)(128)(4,1)S(1)}, s32[]{:S(2)}) async-start(s8[5013504]{0:T(1024)(128)(4,1)} %bitcast.211), calls=%async_computation.19 | async-start | bytes 1638400
  781.6 15.3 %slice-start.1 = ((s8[5013504]{0:T(1024)(128)(4,1)}), s8[819200]{0:T(1024)(128)(4,1)S(1)}, s32[]{:S(2)}) async-start(s8[5013504]{0:T(1024)(128)(4,1)} %bitcast.209), calls=%async_computation.17 | async-start | bytes 1638400
  796.9 13.1 %copy-start.21 = (bf16[2064,288]{0,1:T(8,128)(2,1)S(1)}, bf16[2064,288]{0,1:T(8,128)(2,1)}, u32[]{:S(2)}) copy-start(bf16[2064,288]{0,1:T(8,128)(2,1)} %param.26) | copy-start | bytes 3566596
  803.8 11.6 %copy-start.19 = (bf16[2064,288]{0,1:T(8,128)(2,1)S(1)}, bf16[2064,288]{0,1:T(8,128)(2,1)}, u32[]{:S(2)}) copy-start(bf16[2064,288]{0,1:T(8,128)(2,1)} %param.25) | copy-start | bytes 3566596
  810.0 5.4 copy-start.41
  819.5 3.7 copy-start.35
  819.5 47.6 %copy-start.22 = (bf16[288,1152]{1,0:T(8,128)(2,1)S(1)}, bf16[288,1152]{1,0:T(8,128)(2,1)}, u32[]{:S(2)}) copy-start(bf16[288,1152]{1,0:T(8,128)(2,1)} %param.32) | copy-start | bytes 1990660
  867.1 5.4 copy-start.16
  1113.8 4.6 copy-start.23
  1113.8 5.8 copy-start.17
  (18 other events, 42.1 us)
Sparse Core Ops, SparseCore 0:
  19.0 84.3 reduce-scatter.15
  126.5 39.6 all-gather.5
  250.5 49.8 reduce-scatter.17
  324.2 39.6 all-gather.7
  365.9 39.0 all-gather.9
  415.4 49.8 reduce-scatter.19
  468.4 49.8 reduce-scatter.21
  545.0 39.6 all-gather.11
  695.0 49.8 reduce-scatter.23
  770.2 39.7 all-gather.13
  818.3 295.5 all-reduce.7
where the time goes:
time: 1140 us
  waiting for transfers between devices  601 us (53%)
  matrix products  221 us (19%)
  local copies, waits for them, and re-layouts  152 us (13%)
  blocking collectives  80.5 us (7%)
  other arithmetic  64.8 us (6%)
  between operations  15.4 us (1%)
    unnamed x16, waiting for transfers between devices  249 us
    psum x1, waiting for transfers between devices, body(): lax.psum(g_w_main.astype(jnp.bfloat16), 'dp').astype(jnp.float32)  236 us
    all_gather x2, waiting for transfers between devices, layer_norm(): return (normed, rstd, lax.all_gather(rounded, 'tp', axis=0, tiled=True))  69.8 us
    unnamed x123, local copies, waits for them, and re-layouts  63.8 us
    all_gather x3, waiting for transfers between devices, fold_back(): piece = lax.all_gather(shard, 'tp', axis=0, tiled=True)  46 us
    psum x1, blocking collectives, body(): lax.psum(g_b_skip.astype(jnp.bfloat16), 'dp').astype(jnp.float32)  39.2 us
    dot_general x4, matrix products, fold_back(): jnp.einsum('fc,ct->ft', weight, piece, preferred_element_type=jnp.float32)  32.7 us
    dot_general x1, matrix products, body(): jnp.einsum('dc,dt->ct', w_up, full_two, preferred_element_type=jnp.float32)  32.2 us
  transfers between devices with their start and end apart: 11, of which 10 were waited for; matrix products, arithmetic and copies ran while one was open for 13% of the time, Pallas kernels for 0%

commit v1 on v0

--- a/solution.py
+++ b/solution.py
@@ -260,7 +260,7 @@
     ) = (
         lax.psum(g_w_main.astype(jnp.bfloat16), "dp").astype(jnp.float32),
         lax.psum(g_w_long.astype(jnp.bfloat16), "dp").astype(jnp.float32),
-        lax.psum(g_b_skip.astype(jnp.bfloat16), "dp").astype(jnp.float32),
+        jnp.sum(lax.all_gather(g_b_skip.astype(jnp.bfloat16), "dp"), axis=0).astype(jnp.float32),
         lax.psum(g_ln1_gain.astype(jnp.bfloat16), "dp").astype(jnp.float32),
         lax.psum(g_ln1_bias.astype(jnp.bfloat16), "dp").astype(jnp.float32),
         lax.psum(g_w_qkv.astype(jnp.bfloat16), "dp").astype(jnp.float32),

time: 1140 us -> 1140 us (level)
    unnamed x0 -> x1, blocking collectives: none -> 39.5 us
    psum x1 -> x0, blocking collectives: 39.2 us -> none  [body(): lax.psum(g_b_skip.astype(jnp.bfloat16), 'dp').astype(jnp.float32)]
    unnamed x123 -> x128, local copies, waits for them, and re-layouts: 63.8 us -> 63.8 us
where the time goes in v1:
time: 1140 us
  waiting for transfers between devices  599 us (53%)
  matrix products  219 us (19%)
  local copies, waits for them, and re-layouts  152 us (13%)
  blocking collectives  80.8 us (7%)
  other arithmetic  67.9 us (6%)
  between operations  16.1 us (1%)
    unnamed x16, waiting for transfers between devices  249 us
    psum x1, waiting for transfers between devices, body(): lax.psum(g_w_main.astype(jnp.bfloat16), 'dp').astype(jnp.float32)  234 us
    all_gather x2, waiting for transfers between devices, layer_norm(): return (normed, rstd, lax.all_gather(rounded, 'tp', axis=0, tiled=True))  69.8 us
    unnamed x128, local copies, waits for them, and re-layouts  63.8 us
    all_gather x3, waiting for transfers between devices, fold_back(): piece = lax.all_gather(shard, 'tp', axis=0, tiled=True)  46 us
    unnamed x1, blocking collectives  39.5 us
    dot_general x1, matrix products, body(): jnp.einsum('dc,dt->ct', w_up, full_two, preferred_element_type=jnp.float32)  32.2 us
    dot_general x4, matrix products, fold_back(): jnp.einsum('fc,ct->ft', weight, piece, preferred_element_type=jnp.float32)  30.4 us
  transfers between devices with their start and end apart: 11, of which 10 were waited for; matrix products, arithmetic and copies ran while one was open for 13% of the time, Pallas kernels for 0%

profile of v1, /device:TPU:0, one launch (start us, length us, event | category | flops | bytes accessed | tf_op | source)
XLA Modules:
  0.0 1135.2 jit_solution(6544796627202988883)
XLA Ops:
  7.3 4.6 fusion.123
  11.9 6.9 convolution_add_fusion
  18.9 84.4 %reduce-scatter.16.cloned.1.call-done = f32[288,2064]{1,0:T(8,128)} async-done(((f32[1152,2064]{1,0:T(8,128)}), f32[288,2064]{1,0:T(8,128)}) %reduce-scatter.16.cloned.1.call-update) | async-done | bytes 2377744
  109.4 10.3 all-reduce.4
  126.7 39.5 %all-gather.7.cloned.1.call-done = bf16[1152,2064]{1,0:T(8,128)(2,1)} async-done(((bf16[288,2064]{1,0:T(8,128)(2,1)}), bf16[1152,2064]{1,0:T(8,128)(2,1)}) %all-gather.7.cloned.1.call-update) | async-done | bytes 4755472 | tf_op jit(solution)/shard_map/all_gather | solution.py:35
  166.2 8.2 fusion.83
  176.4 6.6 reshape_squeeze.11
  183.0 6.6 reshape_squeeze.10
  189.6 6.6 reshape_squeeze.9
  203.0 23.4 %while.26 = (s32[]{:T(128)}, bf16[4,4,72,2,258]{4,2,3,1,0:T(8,128)(2,1)}, f32[4,4,2,258]{3,2,1,0:T(2,128)}, bf16[4,4,72,2,258]{4,2,3,1,0:T(8,128)(2,1)}, bf16[4,...) while((s32[]{:T(128)}, bf16[4,4,72,2,258]{4,2,3,1,0:T(8,128)(2,1)}, ...), condition=%wide.region_8.0_spmd, body=%wide.region_5.8_spmd.sunk | while | flops 157770096 | bytes 8231833 | solution.py:174
  230.5 5.1 reshape.91
  235.6 6.4 fusion.62
  242.0 8.4 copy.129
  250.5 50.0 %reduce-scatter.18.cloned.1.call-done = bf16[288,2064]{1,0:T(8,128)(2,1)} async-done(((bf16[1152,2064]{1,0:T(8,128)(2,1)}), bf16[288,2064]{1,0:T(8,128)(2,1)}) %reduce-scatter.18.cloned.1.call-update) | async-done | bytes 1188880
  303.0 4.6 fusion.116
  307.6 10.3 all-reduce.3
  333.6 30.3 %all-gather.9.cloned.1.call-done = bf16[1152,2064]{1,0:T(8,128)(2,1)} async-done(((bf16[288,2064]{1,0:T(8,128)(2,1)}), bf16[1152,2064]{1,0:T(8,128)(2,1)}) %all-gather.9.cloned.1.call-update) | async-done | bytes 4755472 | tf_op jit(solution)/shard_map/all_gather | solution.py:35
  363.9 32.2 %fusion.68 = (bf16[1152,2064]{0,1:T(8,128)(2,1)S(1)}, f32[1152,2064]{0,1:T(8,128)}) fusion(f32[1152]{0:T(1024)S(1)} %copy-done.44, bf16[1152,2064]{1,0:T(8,128)(2,1)} %all-gather.9.cloned.1.call-done, bf16[1152,1152]{1,0:T(8,128)(2,1)S(1)} %copy-done), kind=kOutput, calls=%fused_computation.81 | convolution fusion | flops 5635215360 | bytes 21680640 | tf_op jit(solution)/shard_map/dc,dt->ct/dot_general | solution.py:188
  398.4 8.5 fusion.63
  406.9 8.4 copy.131
  415.3 16.6 %fusion.122 = (bf16[1152]{0:T(1024)(128)(2,1)}, bf16[1152,2064]{0,1:T(8,128)(2,1)S(1)}) fusion(f32[1152,2064]{0,1:T(8,128)} %get-tuple-element.220, bf16[1152,2064]{1,0:T(8,128)(2,1)} %all-gather.11.cloned.1.call-done, bf16[1152,1152]{1,0:T(8,128)(2,1)} %param.44), kind=kOutput, calls=%fused_computation.176 | convolution fusion | flops 5504439296 | bytes 21678336 | tf_op jit(solution)/shard_map/fc,ct->ft/dot_general | solution.py:60
  434.1 8.7 fusion.64
  442.8 8.4 copy.133
  451.4 13.9 %reduce-scatter.20.cloned.1.call-done = bf16[288,2064]{1,0:T(8,128)(2,1)} async-done(((bf16[1152,2064]{1,0:T(8,128)(2,1)}), bf16[288,2064]{1,0:T(8,128)(2,1)}) %reduce-scatter.20.cloned.1.call-update) | async-done | bytes 1188880
  467.9 50.4 %reduce-scatter.22.cloned.1.call-done = bf16[288,2064]{1,0:T(8,128)(2,1)} async-done(((bf16[1152,2064]{1,0:T(8,128)(2,1)}), bf16[288,2064]{1,0:T(8,128)(2,1)}) %reduce-scatter.22.cloned.1.call-update) | async-done | bytes 1188880
  520.9 6.0 fusion.101
  526.9 10.3 all-reduce.2
  537.1 5.0 fusion.117
  544.9 39.8 %all-gather.13.cloned.1.call-done = bf16[1152,2064]{1,0:T(8,128)(2,1)} async-done(((bf16[288,2064]{1,0:T(8,128)(2,1)}), bf16[1152,2064]{1,0:T(8,128)(2,1)}) %all-gather.13.cloned.1.call-update) | async-done | bytes 4755472 | tf_op jit(solution)/shard_map/all_gather | solution.py:57
  584.7 5.3 fusion.92
  590.0 6.2 reshape.92
  601.7 51.4 %while.27 = (s32[]{:T(128)}, bf16[4,4,72,2,258]{4,2,3,1,0:T(8,128)(2,1)}, bf16[4,4,72,2,258]{4,2,3,1,0:T(8,128)(2,1)}, bf16[4,4,72,2,258]{4,2,3,1,0:T(8,128)(2,1...) while((s32[]{:T(128)}, ...), condition=%wide.region_23.24_spmd, body=%wide.region_21.23_spmd.sunk | while | flops 390539744 | bytes 20462064 | solution.py:227
  662.1 5.3 stack_reshape.9
  669.9 5.2 stack_reshape.10
  678.9 7.7 fusion.65
  686.5 8.4 copy.135
  695.0 50.0 %reduce-scatter.24.cloned.1.call-done = bf16[288,2064]{1,0:T(8,128)(2,1)} async-done(((bf16[1152,2064]{1,0:T(8,128)(2,1)}), bf16[288,2064]{1,0:T(8,128)(2,1)}) %reduce-scatter.24.cloned.1.call-update) | async-done | bytes 1188880
  747.5 4.3 fusion.107
  751.9 10.5 all-reduce.1
  762.4 5.1 fusion.119
  770.1 11.5 %convolution_convert_fusion.4 = bf16[1152,1152]{1,0:T(8,128)(2,1)} fusion(bf16[1152,2064]{1,0:T(8,128)(2,1)} %all-gather.9.cloned.1.call-done, bf16[1152,2064]{0,1:T(8,128)(2,1)} %copy-done.48), kind=kOutput, calls=%fused_computation.102 | convolution fusion | flops 5479612416 | bytes 12165120 | tf_op jit(solution)/shard_map/dt,ft->df/dot_general | solution.py:213
  781.6 12.4 %convolution_convert_fusion.3 = bf16[1152,1152]{1,0:T(8,128)(2,1)} fusion(bf16[1152,2064]{0,1:T(8,128)(2,1)} %copy-done.49, bf16[1152,2064]{1,0:T(8,128)(2,1)} %all-gather.11.cloned.1.call-done), kind=kOutput, calls=%fused_computation.101 | convolution fusion | flops 5479612416 | bytes 12165120 | tf_op jit(solution)/shard_map/ft,ct->fc/dot_general | solution.py:66
  796.9 6.9 fusion.108
  803.8 6.2 all-gather.15.cloned.1.call-done
  810.0 5.3 fusion.112
  826.9 39.5 %all-reduce.5 = (bf16[2304]{0:T(1024)(128)(2,1)S(1)}, bf16[288]{0:T(512)(128)(2,1)S(1)}, bf16[288]{0:T(512)(128)(2,1)S(1)}, bf16[288]{0:T(512)(128)(2,1)S(1)}, b...) all-reduce(bf16[2304]{0:T(1024)(128)(2,1)S(1)} %dynamic-update-slic, ...), channel_id=2, replica_groups=mesh['dp'=8,'tp'=4] {'dp'}, use_global_device_ids=true, to_apply=%add | all-reduce | flops 5184 | bytes 20736
  871.2 5.6 convolution_convert_fusion.7
  879.7 234.1 %all-reduce.9.cloned.1.call-done = (bf16[288,1152]{1,0:T(8,128)(2,1)}, bf16[288,1152]{1,0:T(8,128)(2,1)}, bf16[3,1152,288]{1,2,0:T(8,128)(2,1)}, bf16[288,1152]{...) async-done(((bf16[288,1152]{1,0:T(8,128)(2,1)}, bf16[288,1152]{1,0:T(8,128)(2,1)}, bf16[3,1152,288]{1,2,0:T(8,128)(2,1)}, ...) | async-done | bytes 9289744 | tf_op jit(solution)/shard_map/psum | solution.py:261
  (251 shorter events, 192.4 us)
Async XLA Ops:
  7.2 356.7 %copy-start = (bf16[1152,1152]{1,0:T(8,128)(2,1)S(1)}, bf16[1152,1152]{1,0:T(8,128)(2,1)}, u32[]{:S(2)}) copy-start(bf16[1152,1152]{1,0:T(8,128)(2,1)} %param.42) | copy-start | bytes 7962628
  7.2 4.6 copy-start.13
  7.2 96.1 %reduce-scatter.16.cloned.1.call-start = ((), (), s32[]{:S(2)}) async-start(), calls=%async_computation.10 | async-start | bytes 12533760
  7.3 4.6 copy-start.18
  18.8 88.0 %copy-start.28 = (f32[288]{0:T(512)S(1)}, f32[288]{0:T(512)}, u32[]{:S(2)}) copy-start(f32[288]{0:T(512)} %param.34) | copy-start | bytes 3460
  18.8 101.5 %copy-start.31 = (f32[288]{0:T(512)S(1)}, f32[288]{0:T(512)}, u32[]{:S(2)}) copy-start(f32[288]{0:T(512)} %param.35) | copy-start | bytes 3460
  18.9 101.5 %copy-start.34 = (f32[288]{0:T(512)S(1)}, f32[288]{0:T(512)}, u32[]{:S(2)}) copy-start(f32[288]{0:T(512)} %param.36) | copy-start | bytes 3460
  18.9 147.4 %all-gather.7.cloned.1.call-start = ((), (), s32[]{:S(2)}) async-start(), calls=%async_computation.5 | async-start | bytes 6266880 | tf_op jit(solution)/shard_map/all_gather | solution.py:35
  126.4 174.0 %reduce-scatter.18.cloned.1.call-start = ((), (), s32[]{:S(2)}) async-start(), calls=%async_computation.11 | async-start | bytes 6266880
  226.4 9.2 copy-start.42
  250.4 52.6 %copy-start.35 = (f32[288]{0:T(512)S(1)}, f32[288]{0:T(512)}, u32[]{:S(2)}) copy-start(f32[288]{0:T(512)} %param.39) | copy-start | bytes 3460
  250.4 113.5 %all-gather.9.cloned.1.call-start = ((), (), s32[]{:S(2)}) async-start(), calls=%async_computation.6 | async-start | bytes 6266880 | tf_op jit(solution)/shard_map/all_gather | solution.py:35
  303.0 14.9 %copy-start.30 = (f32[288]{0:T(512)S(1)}, f32[288]{0:T(512)}, u32[]{:S(2)}) copy-start(f32[288]{0:T(512)} %param.40) | copy-start | bytes 3460
  303.0 14.9 %copy-start.36 = (f32[288]{0:T(512)S(1)}, f32[288]{0:T(512)}, u32[]{:S(2)}) copy-start(f32[288]{0:T(512)} %param.41) | copy-start | bytes 3460
  324.1 91.3 %all-gather.11.cloned.1.call-start = ((), (), s32[]{:S(2)}) async-start(), calls=%async_computation.7 | async-start | bytes 6266880 | tf_op jit(solution)/shard_map/all_gather | solution.py:57
  328.0 35.9 %copy-start.44 = (f32[1152]{0:T(1024)S(1)}, f32[1152]{0:T(1024)}, u32[]{:S(2)}) copy-start(f32[1152]{0:T(1024)} %param.43) | copy-start | bytes 13828
  333.6 131.7 %reduce-scatter.20.cloned.1.call-start = ((), (), s32[]{:S(2)}) async-start(), calls=%async_computation.12 | async-start | bytes 6266880
  363.9 34.5 %copy-start.40 = (bf16[1152,1152]{1,0:T(8,128)(2,1)S(1)}, bf16[1152,1152]{1,0:T(8,128)(2,1)}, u32[]{:S(2)}) copy-start(bf16[1152,1152]{1,0:T(8,128)(2,1)} %param.44) | copy-start | bytes 7962628
  415.3 103.0 %reduce-scatter.22.cloned.1.call-start = ((), (), s32[]{:S(2)}) async-start(), calls=%async_computation.13 | async-start | bytes 6266880
  451.2 69.7 %copy-start.37 = (f32[288]{0:T(512)S(1)}, f32[288]{0:T(512)}, u32[]{:S(2)}) copy-start(f32[288]{0:T(512)} %param.45) | copy-start | bytes 3460
  451.2 133.4 %all-gather.13.cloned.1.call-start = ((), (), s32[]{:S(2)}) async-start(), calls=%async_computation.8 | async-start | bytes 6266880 | tf_op jit(solution)/shard_map/all_gather | solution.py:57
  520.9 16.3 %copy-start.2 = (bf16[2064,288]{1,0:T(8,128)(2,1)S(1)}, bf16[2064,288]{1,0:T(8,128)(2,1)}, u32[]{:S(2)}) copy-start(bf16[2064,288]{1,0:T(8,128)(2,1)} %copy.114) | copy-start | bytes 3566596
  542.2 42.5 %copy-start.43 = (bf16[288,1152]{1,0:T(8,128)(2,1)S(1)}, bf16[288,1152]{1,0:T(8,128)(2,1)}, u32[]{:S(2)}) copy-start(bf16[288,1152]{1,0:T(8,128)(2,1)} %param.38) | copy-start | bytes 1990660
  544.8 200.1 %reduce-scatter.24.cloned.1.call-start = ((), (), s32[]{:S(2)}) async-start(), calls=%async_computation.14 | async-start | bytes 6266880
  657.9 9.4 copy-start.7
  669.9 5.2 copy-start.9
  694.9 52.6 %copy-start.25 = (f32[2064]{0:T(1024)S(1)}, f32[2064]{0:T(1024)}, u32[]{:S(2)}) copy-start(f32[2064]{0:T(1024)} %copy-done.24) | copy-start | bytes 24772
  694.9 52.6 %copy-start.27 = (f32[2064]{0:T(1024)S(1)}, f32[2064]{0:T(1024)}, u32[]{:S(2)}) copy-start(f32[2064]{0:T(1024)} %copy-done.26) | copy-start | bytes 24772
  694.9 52.6 %copy-start.29 = (f32[288]{0:T(512)S(1)}, f32[288]{0:T(512)}, u32[]{:S(2)}) copy-start(f32[288]{0:T(512)} %param.34) | copy-start | bytes 3460
  694.9 52.6 %copy-start.32 = (f32[288]{0:T(512)S(1)}, f32[288]{0:T(512)}, u32[]{:S(2)}) copy-start(f32[288]{0:T(512)} %param.35) | copy-start | bytes 3460
  694.9 67.5 %copy-start.4 = (bf16[288,2064]{0,1:T(8,128)(2,1)S(1)}, bf16[288,2064]{0,1:T(8,128)(2,1)}, u32[]{:S(2)}) copy-start(bf16[288,2064]{0,1:T(8,128)(2,1)} %get-tuple-element.203) | copy-start | bytes 3566596
  694.9 115.0 %all-gather.15.cloned.1.call-start = ((), (), s32[]{:S(2)}) async-start(), calls=%async_computation.9 | async-start | bytes 6266880 | tf_op jit(solution)/shard_map/all_gather | solution.py:57
  770.1 343.7 %all-reduce.9.cloned.1.call-start = ((), (), s32[]{:S(2)}) async-start(), calls=%async_computation.15 | async-start | bytes 18579456 | tf_op jit(solution)/shard_map/psum | solution.py:261
  770.1 23.9 %slice-start.2 = ((s8[5013504]{0:T(1024)(128)(4,1)}), s8[4194304]{0:T(1024)(128)(4,1)S(1)}, s32[]{:S(2)}) async-start(s8[5013504]{0:T(1024)(128)(4,1)} %bitcast.212), calls=%async_computation.18 | async-start | bytes 8388608
  770.1 26.7 %slice-start = ((s8[5013504]{0:T(1024)(128)(4,1)}), s8[4194304]{0:T(1024)(128)(4,1)S(1)}, s32[]{:S(2)}) async-start(s8[5013504]{0:T(1024)(128)(4,1)} %bitcast.210), calls=%async_computation.16 | async-start | bytes 8388608
  781.6 12.4 %copy-start.16 = (bf16[288,2064]{1,0:T(8,128)(2,1)S(1)}, bf16[288,2064]{1,0:T(8,128)(2,1)}, u32[]{:S(2)}) copy-start(bf16[288,2064]{1,0:T(8,128)(2,1)} %reshape.91) | copy-start | bytes 3566596
  781.6 12.4 %slice-start.3 = ((s8[5013504]{0:T(1024)(128)(4,1)}), s8[819200]{0:T(1024)(128)(4,1)S(1)}, s32[]{:S(2)}) async-start(s8[5013504]{0:T(1024)(128)(4,1)} %bitcast.212), calls=%async_computation.19 | async-start | bytes 1638400
  781.6 15.3 %slice-start.1 = ((s8[5013504]{0:T(1024)(128)(4,1)}), s8[819200]{0:T(1024)(128)(4,1)S(1)}, s32[]{:S(2)}) async-start(s8[5013504]{0:T(1024)(128)(4,1)} %bitcast.210), calls=%async_computation.17 | async-start | bytes 1638400
  796.9 13.1 %copy-start.19 = (bf16[2064,288]{0,1:T(8,128)(2,1)S(1)}, bf16[2064,288]{0,1:T(8,128)(2,1)}, u32[]{:S(2)}) copy-start(bf16[2064,288]{0,1:T(8,128)(2,1)} %param.26) | copy-start | bytes 3566596
  803.8 11.6 %copy-start.17 = (bf16[2064,288]{0,1:T(8,128)(2,1)S(1)}, bf16[2064,288]{0,1:T(8,128)(2,1)}, u32[]{:S(2)}) copy-start(bf16[2064,288]{0,1:T(8,128)(2,1)} %param.25) | copy-start | bytes 3566596
  810.0 5.3 copy-start.39
  820.0 6.9 copy-start.33
  820.0 51.1 %copy-start.20 = (bf16[288,1152]{1,0:T(8,128)(2,1)S(1)}, bf16[288,1152]{1,0:T(8,128)(2,1)}, u32[]{:S(2)}) copy-start(bf16[288,1152]{1,0:T(8,128)(2,1)} %param.32) | copy-start | bytes 1990660
  825.3 51.5 %slice-start.4 = ((s8[5013504]{0:T(1024)(128)(4,1)}), s8[819200]{0:T(1024)(128)(4,1)S(1)}, s32[]{:S(2)}) async-start(s8[5013504]{0:T(1024)(128)(4,1)} %bitcast.214), calls=%async_computation.20 | async-start | bytes 1638400
  871.2 5.6 copy-start.14
  871.2 5.6 slice-start.5
  1113.8 4.6 copy-start.21
  1113.8 5.8 copy-start.15
  (19 other events, 44.7 us)
Sparse Core Ops, SparseCore 0:
  18.9 84.3 reduce-scatter.15
  126.5 39.6 all-gather.6
  250.5 49.8 reduce-scatter.17
  324.2 39.6 all-gather.8
  365.9 39.0 all-gather.10
  415.4 49.8 reduce-scatter.19
  468.4 49.8 reduce-scatter.21
  545.0 39.6 all-gather.12
  695.1 49.8 reduce-scatter.23
  770.2 39.7 all-gather.14
  818.3 295.5 all-reduce.8
